TPU v7x, 256 devices: a whole 4x4x8 slice. The times are simulated.
256 devices in a mesh: rep: 8 (over x_lo, y), ep: 32 (over x_hi, z, core).
Axes of the slice: x: 4 (x_hi: 2, x_lo: 2; x = x_hi * 2 + x_lo), y: 4, z: 8, core: 2. Of those that a mesh axis runs over, the one named last changes fastest.
Arguments:
- hidden: bfloat16 [4, 8192, 2, 2048], P(None, ('rep', 'ep')), may hold values from -6 to 6
- out_grad: bfloat16 [4, 8192, 7168], P(None, ('rep', 'ep')), may hold values from -0.5 to 0.5
- route_weight: float32 [4, 8192, 2], P(None, ('rep', 'ep')), may hold values from 0.05 to 1
- expert_ids: int32 [4, 8192, 2], P(None, ('rep', 'ep')), may hold values from 0 to 31, as said below
Outputs:
- grad_down: bfloat16 [32, 2048, 7168], P('ep', None, 'rep')
- expert_load: float32 [32], replicated
Inputs may be any that keep to these rules, and one draw needn't show every extreme that they name: `expert_ids`: in each micro-batch the 32 tokens of one device (aligned blocks of 32 tokens) name no expert in more than 4 pairs, and some expert is named in exactly 4; the 2 experts of a token differ.
All inputs are finite; a program needn't handle non-finite values.
Results may differ from a plain program's by a relative error of at most 0.0049.
Values may be sent and summed in bfloat16 or wider, within the bound.
A program may use at most 192 MiB of HBM per device.

v0:
```python
import functools

import jax
import jax.numpy as jnp
from jax import lax
from jax.experimental import pallas as pl
from jax.experimental.pallas import tpu as pltpu
from jax.sharding import Mesh
from jax.sharding import PartitionSpec as P

REP_EP = ("rep_0", "rep_1", "ep_0", "ep_1", "ep_2")
EP = ("ep_0", "ep_1", "ep_2")
REP = ("rep_0", "rep_1")
MESH = pl.DeviceIdType.MESH
NX, NY, NZ, NC = 4, 4, 8, 2
NE = NZ * NC
NQ = NX * NY
ZC = [(1, 0), (7, 0), (1, 1), (7, 1), (2, 0), (6, 0), (2, 1), (6, 1), (3, 0), (5, 0), (3, 1), (5, 1), (4, 0), (4, 1), (0, 1)]
GROUP_DY = [0, 1, 3, 2]


def kernel(hid_ref, slot_ref, meta_ref, og_ref, out_ref, load_ref,
           graw, meta, gsend, gall, hp, hz, hzt, ht, acc, cnt, cnt_all,
           s_send, s_meta, s_graw, s_gz, s_hz, s_hx, s_hy, s_cnt, s_local):
    cap = hp.shape[2]
    ff = hzt.shape[1]
    cols = graw.shape[3]
    rows = NE * cap
    toks = graw.shape[1] * graw.shape[2]
    xlo, y = lax.axis_index("rep_0"), lax.axis_index("rep_1")
    xhi, z, core = lax.axis_index("ep_0"), lax.axis_index("ep_1"), lax.axis_index("ep_2")
    x = xhi * 2 + xlo
    me = z * NC + core

    def plane(dx, dy):
        x2, y2 = lax.rem(x + dx, NX), lax.rem(y + dy, NY)
        return x2, y2, {"rep_0": lax.rem(x2, 2), "rep_1": y2, "ep_0": x2 // 2}

    def zc(dz, dc):
        z2, c2 = lax.rem(z + dz, NZ), lax.rem(core + dc, NC)
        return z2 * NC + c2, {"ep_1": z2, "ep_2": c2}

    def send(src, dst, send_sem, recv_sem, dev):
        pltpu.make_async_remote_copy(
            src_ref=src, dst_ref=dst, send_sem=send_sem, recv_sem=recv_sem, device_id=dev, device_id_type=MESH
        ).start()

    def wait(ref, sem):
        pltpu.make_async_copy(ref, ref, sem).wait()

    barrier = pltpu.get_barrier_semaphore()
    for dy in range(NY):
        for dx in range(NX):
            if dx or dy:
                pl.semaphore_signal(barrier, inc=1, device_id=plane(dx, dy)[2], device_id_type=MESH)
    for dz, dc in ZC:
        pl.semaphore_signal(barrier, inc=1, device_id=zc(dz, dc)[1], device_id_type=MESH)
    pl.semaphore_wait(barrier, NQ - 1 + NE - 1)

    for group in range(NY):
        dy = (NY - GROUP_DY[group]) % NY
        for dx in (0, 1, 3, 2):
            if not (dx or dy):
                continue
            _, y2, dev = plane(dx, dy)
            send(meta_ref, meta.at[group * NX + x], s_send.at[0], s_meta, dev)
        for dx in (0, 1, 3, 2):
            if not (dx or dy):
                continue
            x2, y2, dev = plane(dx, dy)
            at = pl.multiple_of((lax.rem(x2, 2) * NY + y2) * cols, 128)
            send(og_ref.at[:, :, pl.ds(at, cols)], graw.at[group * NX + x], s_send.at[1], s_graw.at[group], dev)
    mine = pl.multiple_of((xlo * NY + y) * cols, 128)
    own_g = pltpu.make_async_copy(og_ref.at[:, :, pl.ds(mine, cols)], graw.at[x], s_local.at[0])
    own_g.start()
    own_m = pltpu.make_async_copy(meta_ref, meta.at[x], s_local.at[1])
    own_m.start()

    half = NE * cap
    pairs = hid_ref.shape[0]
    for i in range(2):
        sel = jnp.where(
            lax.broadcasted_iota(jnp.int32, (half, pairs), 0) + i * half == slot_ref[...], 1.0, 0.0
        ).astype(jnp.bfloat16)
        for c in range(0, ff, 512):
            packed = jnp.dot(sel, hid_ref[:, c:c + 512], preferred_element_type=jnp.float32)
            hp[i, :, :, c:c + 512] = packed.astype(jnp.bfloat16).reshape(NE, cap, 512)
    own_m.wait()
    own_g.wait()
    wait(meta.at[pl.ds(0, NQ - 1)], s_meta)
    total = meta[0]
    for q in range(1, NQ):
        total = total + meta[q]
    cnt[...] = total
    for dz, dc in ZC:
        e, dev = zc(dz, dc)
        send(hp.at[:, e], hz.at[:, me], s_send.at[2], s_hz, dev)
    own_h = pltpu.make_async_copy(hp.at[:, me], hz.at[:, me], s_local.at[2])
    own_h.start()

    def pack_and_send(group):
        if group:
            wait(graw.at[pl.ds(group * NX, NX)], s_graw.at[group])
        else:
            wait(graw.at[pl.ds(0, NX - 1)], s_graw.at[0])
        slot_of_row = (lax.broadcasted_iota(jnp.int32, (rows, toks), 0) + xhi * rows).astype(jnp.float32)
        for xs in range(NX):
            q = group * NX + xs
            info = meta[q]
            first = slot_of_row == info[0:1, :]
            second = slot_of_row == info[1:2, :]
            weights = jnp.where(first, info[2:3, :], jnp.where(second, info[3:4, :], 0.0))
            weight = jnp.sum(weights, axis=1, keepdims=True)
            sel = jnp.where(first | second, 1.0, 0.0).astype(jnp.bfloat16)
            raw = graw[q].reshape(toks, cols)
            packed = jnp.dot(sel, raw, preferred_element_type=jnp.float32) * weight
            gsend[q] = packed.astype(jnp.bfloat16).reshape(NE, cap, cols)
        part = pl.ds(group * NX, NX)
        for dz, dc in ZC:
            e, dev = zc(dz, dc)
            send(gsend.at[part, e], gall.at[part, me], s_send.at[3], s_gz.at[group], dev)
        own = pltpu.make_async_copy(gsend.at[part, me], gall.at[part, me], s_local.at[3 + group])
        own.start()
        return own

    owns = [pack_and_send(0), pack_and_send(1), pack_and_send(2)]

    own_h.wait()
    wait(hz.at[:, pl.ds(0, NE - 1)], s_hz)
    eye = jnp.where(
        lax.broadcasted_iota(jnp.int32, (256, 256), 0) == lax.broadcasted_iota(jnp.int32, (256, 256), 1), 1.0, 0.0
    ).astype(jnp.bfloat16)
    for i in range(2):
        for c in range(0, ff, 256):
            block = hz[i, :, :, c:c + 256].reshape(rows, 256)
            turned = lax.dot_general(eye, block, (((1,), (1,)), ((), ())), preferred_element_type=jnp.float32)
            hzt[i, c:c + 256, :] = turned.astype(jnp.bfloat16)
    for dz, dc in ZC:
        e, dev = zc(dz, dc)
        send(cnt, cnt_all.at[me], s_send.at[4], s_cnt, dev)
    for dx in (1, 3, 2):
        x2, _, dev = plane(dx, 0)
        send(hzt.at[x2 // 2], ht.at[x], s_send.at[5], s_hx.at[x], dev)
    own_t = pltpu.make_async_copy(hzt.at[xhi], ht.at[x], s_local.at[7])
    own_t.start()

    owns.append(pack_and_send(3))

    _, _, up = plane(0, 1)
    _, _, down = plane(0, 3)
    hf = ff // 2

    def to_row(xs):
        send(ht.at[xs], ht.at[2 * NX + xs], s_send.at[6], s_hy.at[0, xs], up)
        send(ht.at[xs], ht.at[NX + xs], s_send.at[6], s_hy.at[1, xs], down)

    own_t.wait()
    to_row(x)
    for dx in (1, 3, 2):
        xs = lax.rem(x + dx, NX)
        wait(ht.at[xs], s_hx.at[xs])
        to_row(xs)
    for dx in (0, 1, 3, 2):
        xs = lax.rem(x + dx, NX)
        wait(ht.at[2 * NX + xs], s_hy.at[0, xs])
        send(ht.at[2 * NX + xs, pl.ds(0, hf)], ht.at[3 * NX + xs, pl.ds(0, hf)], s_send.at[7], s_hy.at[2, xs], up)
        wait(ht.at[NX + xs], s_hy.at[1, xs])
        send(ht.at[NX + xs, pl.ds(hf, hf)], ht.at[3 * NX + xs, pl.ds(hf, hf)], s_send.at[7], s_hy.at[3, xs], down)

    tile = 512
    for group in range(NY):
        owns[group].wait()
        wait(gall.at[pl.ds(group * NX, NX), pl.ds(0, NE - 1)], s_gz.at[group])
        if group == NY - 1:
            for xs in range(NX):
                wait(ht.at[3 * NX + xs, pl.ds(0, hf)], s_hy.at[2, xs])
                wait(ht.at[3 * NX + xs, pl.ds(hf, hf)], s_hy.at[3, xs])

        @pl.loop(0, ff // tile)
        def _(m):
            at = pl.ds(pl.multiple_of(m * tile, tile), tile)
            part = None
            for xs in range(NX):
                q = group * NX + xs
                term = jnp.dot(ht[q, at, :], gall[q].reshape(rows, cols), preferred_element_type=jnp.float32)
                part = term if part is None else part + term
            if group == 0:
                acc[at, :] = part
            elif group < NY - 1:
                acc[at, :] += part
            else:
                out_ref[0, at, :] = (acc[at, :] + part).astype(out_ref.dtype)

    wait(cnt_all.at[pl.ds(0, NE - 1)], s_cnt)
    cnt_all[me] = cnt[...]
    loads = cnt_all[0]
    for e in range(1, NE):
        loads = loads + cnt_all[e]
    load_ref[...] = loads

    wait(meta.at[pl.ds(0, NQ - 1)], s_send.at[0])
    wait(graw.at[pl.ds(0, NQ - 1)], s_send.at[1])
    wait(hz.at[:, pl.ds(0, NE - 1)], s_send.at[2])
    wait(gall.at[:, pl.ds(0, NE - 1)], s_send.at[3])
    wait(cnt_all.at[pl.ds(0, NE - 1)], s_send.at[4])
    wait(ht.at[pl.ds(0, NX - 1)], s_send.at[5])
    wait(ht.at[pl.ds(0, 2 * NX)], s_send.at[6])
    wait(ht.at[pl.ds(0, NX)], s_send.at[7])


def body(hidden, out_grad, route_weight, expert_ids):
    micro, tokens, picks, ff = hidden.shape
    width = out_grad.shape[2]
    experts = lax.axis_size(EP)
    replicas = lax.axis_size(REP)
    cols = width // replicas
    limit = 2 * tokens * picks // experts
    cap = micro * limit
    toks = micro * tokens
    ids = expert_ids.reshape(micro, tokens * picks)
    order = jnp.arange(tokens * picks, dtype=jnp.int32)
    earlier = (ids[:, :, None] == ids[:, None, :]) & (order[None, None, :] < order[None, :, None])
    position = jnp.sum(earlier.astype(jnp.int32), axis=2)
    slot = ids * cap + jnp.arange(micro, dtype=jnp.int32)[:, None] * limit + position
    by_token = slot.reshape(toks, picks).T.astype(jnp.float32)
    weights = route_weight.reshape(toks, picks).T
    tally = jnp.sum(
        (expert_ids.reshape(toks * picks)[None, :] == jnp.arange(toks, dtype=jnp.int32)[:, None]).astype(jnp.float32),
        axis=1,
    )
    meta = jnp.concatenate([by_token, weights, tally[None, :], jnp.zeros((3, toks), jnp.float32)], axis=0)
    vmem = pl.BlockSpec(memory_space=pltpu.VMEM)
    bf16 = jnp.bfloat16
    dma = pltpu.SemaphoreType.DMA
    grad, load = pl.pallas_call(
        kernel,
        out_shape=(
            jax.ShapeDtypeStruct((1, ff, cols), bf16),
            jax.ShapeDtypeStruct((8, toks), jnp.float32),
        ),
        in_specs=[vmem, vmem, vmem, pl.BlockSpec(memory_space=pl.ANY)],
        out_specs=(vmem, vmem),
        scratch_shapes=[
            pltpu.VMEM((NQ, micro, tokens, cols), bf16),
            pltpu.VMEM((NQ, 8, toks), jnp.float32),
            pltpu.VMEM((NQ, NE, cap, cols), bf16),
            pltpu.VMEM((NQ, NE, cap, cols), bf16),
            pltpu.VMEM((2, NE, cap, ff), bf16),
            pltpu.VMEM((2, NE, cap, ff), bf16),
            pltpu.VMEM((2, ff, NE * cap), bf16),
            pltpu.VMEM((NQ, ff, NE * cap), bf16),
            pltpu.VMEM((ff, cols), jnp.float32),
            pltpu.VMEM((8, toks), jnp.float32),
            pltpu.VMEM((NE, 8, toks), jnp.float32),
            dma((8,)),
            dma,
            dma((NY,)),
            dma((NY,)),
            dma,
            dma((NX,)),
            dma((4, NX)),
            dma,
            dma((8,)),
        ],
        compiler_params=pltpu.CompilerParams(
            collective_id=0, has_side_effects=True, vmem_limit_bytes=66 * 1024 * 1024 - 4 * 1024 * 1024
        ),
    )(hidden.reshape(toks * picks, ff), slot.reshape(1, toks * picks), meta, out_grad)
    expert_load = load[4, :experts] / float(micro * tokens * replicas * picks)
    return grad, expert_load


def solution(mesh):
    finer = Mesh(mesh.devices.reshape(2, 4, 2, 8, 2), REP_EP)
    placed = (
        P(None, REP_EP, None, None),
        P(None, REP_EP, None),
        P(None, REP_EP, None),
        P(None, REP_EP, None),
    )
    return jax.shard_map(
        body, mesh=finer, in_specs=placed, out_specs=(P(EP, None, REP), P()), check_vma=False
    )
```

profile of v0, /device:TPU:1, one launch (start us, length us, event | category | flops | bytes accessed | tf_op | source)
XLA Modules:
  0.0 280.8 jit_solution(4326902321524252201)
XLA Ops:
  0.6 0.1 pad.3.clone
  0.7 0.1 add.43
  0.8 0.1 add.44
  0.9 0.1 add.39
  0.9 0.1 add.40
  1.0 0.7 broadcast_multiply_fusion
  1.7 0.1 mul.34
  1.8 0.7 copy.23
  2.5 0.1 reshape.78
  2.6 0.8 copy.18
  3.4 0.1 copy.19
  3.5 0.2 convert_reduce_fusion.1
  3.7 0.1 reduce_sum.23
  3.8 0.1 copy.17
  3.9 0.1 mul.32
  4.0 0.6 add_add_fusion.slot_ref
  4.6 0.1 reduce_sum.24
  4.7 0.1 copy.22
  4.8 0.8 copy.24
  5.6 0.1 eq.34
  5.8 0.1 convert_reduce_fusion
  5.9 0.7 maximum_maximum_fusion.meta_ref
  6.5 2.2 reshape.77.hid_ref
  8.8 266.7 %shard_map.59 = (bf16[1,2048,896]{2,1,0:T(8,128)(2,1)}, f32[8,128]{1,0:T(8,128)}) custom-call(bf16[256,2048]{1,0:T(8,128)(2,1)} %reshape.77.hid_ref, s32[1,256]{1,0:T(1,128)} %add_add_fusion.slot_ref, f32[8,128]{1,0:T(8,128)} %maximum_maximum_fusion.meta_ref, bf16[4,32,7168]{2,1,0:T(8,128)(2,1)} %og_ref.1), custom_call_target="tpu_custom_call" | custom-call | tf_op jit(solution)/shard_map/pallas_call | solution.py:235
  275.5 1.2 multiply_bitcast_fusion
  276.7 4.2 %copy.26 = bf16[1,2048,896]{2,1,0:T(8,128)(2,1)} copy(bf16[1,2048,896]{2,1,0:T(8,128)(2,1)} %get-tuple-element.8) | data formatting | bytes 7340032
  (5 shorter events, 0.0 us)
where the time goes:
time: 283 us; the launch traced here: 281 us
  Pallas kernels  267 us (94%)
  local copies, waits for them, and re-layouts  9.96 us (4%)
  other arithmetic  3.51 us (1%)
    pallas_call x1, Pallas kernels, body(): pl.pallas_call(kernel, out_shape=(jax.ShapeDtypeStruct((1, ff, cols), bf1...  267 us
    unnamed x4, local copies, waits for them, and re-layouts  6.45 us

commit v1 on v0

--- a/solution.py
+++ b/solution.py
@@ -60,10 +60,10 @@
     for group in range(NY):
         dy = (NY - GROUP_DY[group]) % NY
         for dx in (0, 1, 3, 2):
-            if not (dx or dy):
-                continue
-            _, y2, dev = plane(dx, dy)
-            send(meta_ref, meta.at[group * NX + x], s_send.at[0], s_meta, dev)
+            if dx or dy:
+                send(meta_ref, meta.at[group * NX + x], s_send.at[0], s_meta, plane(dx, dy)[2])
+    for group in range(NY):
+        dy = (NY - GROUP_DY[group]) % NY
         for dx in (0, 1, 3, 2):
             if not (dx or dy):
                 continue
@@ -87,16 +87,16 @@
             hp[i, :, :, c:c + 512] = packed.astype(jnp.bfloat16).reshape(NE, cap, 512)
     own_m.wait()
     own_g.wait()
+    for dz, dc in ZC:
+        e, dev = zc(dz, dc)
+        send(hp.at[:, e], hz.at[:, me], s_send.at[2], s_hz, dev)
+    own_h = pltpu.make_async_copy(hp.at[:, me], hz.at[:, me], s_local.at[2])
+    own_h.start()
     wait(meta.at[pl.ds(0, NQ - 1)], s_meta)
     total = meta[0]
     for q in range(1, NQ):
         total = total + meta[q]
     cnt[...] = total
-    for dz, dc in ZC:
-        e, dev = zc(dz, dc)
-        send(hp.at[:, e], hz.at[:, me], s_send.at[2], s_hz, dev)
-    own_h = pltpu.make_async_copy(hp.at[:, me], hz.at[:, me], s_local.at[2])
-    own_h.start()
 
     def pack_and_send(group):
         if group:

time: 283 us -> 242 us (0.86)
  Pallas kernels: 267 us -> 227 us
    pallas_call x1, Pallas kernels: 267 us -> 227 us  [body(): pl.pallas_call(kernel, out_shape=(jax.ShapeDtypeStruct((1, ff, cols), bf1...]
where the time goes in v1:
time: 242 us; the launch traced here: 241 us
  Pallas kernels  227 us (94%)
  local copies, waits for them, and re-layouts  9.96 us (4%)
  other arithmetic  3.51 us (1%)
    pallas_call x1, Pallas kernels, body(): pl.pallas_call(kernel, out_shape=(jax.ShapeDtypeStruct((1, ff, cols), bf1...  227 us
    unnamed x4, local copies, waits for them, and re-layouts  6.45 us

profile of v1, /device:TPU:1, one launch (start us, length us, event | category | flops | bytes accessed | tf_op | source)
XLA Modules:
  0.0 241.4 jit_solution(3461288248953751456)
XLA Ops:
  0.6 0.1 pad.3.clone
  0.7 0.1 add.43
  0.8 0.1 add.44
  0.9 0.1 add.39
  0.9 0.1 add.40
  1.0 0.7 broadcast_multiply_fusion
  1.7 0.1 mul.34
  1.8 0.7 copy.23
  2.5 0.1 reshape.78
  2.6 0.8 copy.18
  3.4 0.1 copy.19
  3.5 0.2 convert_reduce_fusion.1
  3.7 0.1 reduce_sum.23
  3.8 0.1 copy.17
  3.9 0.1 mul.32
  4.0 0.6 add_add_fusion.slot_ref
  4.6 0.1 reduce_sum.24
  4.7 0.1 copy.22
  4.8 0.8 copy.24
  5.6 0.1 eq.34
  5.8 0.1 convert_reduce_fusion
  5.9 0.7 maximum_maximum_fusion.meta_ref
  6.5 2.2 reshape.77.hid_ref
  8.8 227.2 %shard_map.59 = (bf16[1,2048,896]{2,1,0:T(8,128)(2,1)}, f32[8,128]{1,0:T(8,128)}) custom-call(bf16[256,2048]{1,0:T(8,128)(2,1)} %reshape.77.hid_ref, s32[1,256]{1,0:T(1,128)} %add_add_fusion.slot_ref, f32[8,128]{1,0:T(8,128)} %maximum_maximum_fusion.meta_ref, bf16[4,32,7168]{2,1,0:T(8,128)(2,1)} %og_ref.1), custom_call_target="tpu_custom_call" | custom-call | tf_op jit(solution)/shard_map/pallas_call | solution.py:235
  236.0 1.2 multiply_bitcast_fusion
  237.2 4.2 %copy.26 = bf16[1,2048,896]{2,1,0:T(8,128)(2,1)} copy(bf16[1,2048,896]{2,1,0:T(8,128)(2,1)} %get-tuple-element.8) | data formatting | bytes 7340032
  (5 shorter events, 0.0 us)
